TPU v7x, 256 devices: a whole 4x4x8 slice. The times are simulated.
256 devices in a mesh: seq: 32 (over y, x, core), vocab: 8 (over z).
Axes of the slice: x: 4, y: 4, z: 8, core: 2. Of those that a mesh axis runs over, the one named last changes fastest.
Arguments:
- hidden: bfloat16 [4096, 8192], P('seq'), may hold values from -120 to 120
- head: bfloat16 [8192, 65536], P(None, ('seq', 'vocab')), may hold values from -0.5 to 0.5
- mask: int32 [4096], P('seq'), may hold values from 0 to 1, as said below
Outputs:
- positionwise_uncertainty: float32 [4096], P('seq')
- average_uncertainty_reward: float32 [], replicated
- derivative_wrt_latent_vectors: bfloat16 [4096, 8192], P('seq', 'vocab')
Inputs may be any that keep to these rules, and one draw needn't show every extreme that they name: Among the 128 tokens of one index of seq at least half of 16 and at most 16 have mask 1, and the last index of seq has exactly 16; later indices have no fewer than earlier ones.
All inputs are finite; a program needn't handle non-finite values.
Results may differ from a plain program's by a relative error of at most 0.019.
Values may be sent and summed in bfloat16 or wider, within the bound.
A program may use at most 64 MiB of HBM per device.

v0:
```python
import jax
import jax.numpy as jnp
from jax import lax
from jax.sharding import Mesh
from jax.sharding import PartitionSpec as P

ACT_DEV = 16
SEQ = ("seq_0", "seq_1", "seq_2")
SEQ_VOCAB = ("seq_0", "seq_1", "seq_2", "vocab")


def gathered_once(array, axis):
    leaves = jax.tree.leaves(array)
    sequence = sorted(range(len(leaves)), key=lambda k: -leaves[k].size)
    width = (1, *leaves[sequence[0]].shape)[-1]
    lines = [
        jnp.pad(leaves[k].reshape(-1), (0, -leaves[k].size % width)).reshape(-1, width)
        for k in sequence
    ]
    both, at, found = (lax.all_gather(jnp.concatenate(lines), axis), 0, {})
    for k, line in zip(sequence, lines):
        slab = both[:, at : at + len(line)].reshape(len(both), -1)
        found[k] = slab[:, : leaves[k].size].reshape(-1, *leaves[k].shape)
        at += len(line)
    numbers = iter(range(len(leaves)))
    return jax.tree.map(lambda _: found[next(numbers)], array)


def combined_by_axis(array, axes, combine):
    for axis in axes:
        pieces = gathered_once(array, axis)
        array = jax.tree.map(lambda part: part[0], pieces)
        for k in range(1, lax.axis_size(axis)):
            array = combine(array, jax.tree.map(lambda part: part[k], pieces))
    return array


def cut_along(array, dim, devices):
    before, after = (array.shape[:dim], array.shape[dim + 1 :])
    return jnp.moveaxis(array.reshape(*before, devices, -1, *after), dim, 0)


def sent_and_summed(array, axis, dim):
    pieces = cut_along(array, dim, lax.axis_size(axis))
    arrived = lax.all_to_all(pieces, axis, split_axis=0, concat_axis=0, tiled=True)
    return arrived.astype(jnp.float32).sum(axis=0)


def from_everyone(array, axis):
    devices = lax.axis_size(axis)
    return lax.all_to_all(
        jnp.broadcast_to(array[None], (devices, *array.shape)), axis, 0, 0, tiled=True
    )


def taken_together(array, axis):
    return from_everyone(array, axis).sum(axis=0)


def packed_total(arrays, axis):
    ends = [0]
    for a in arrays:
        ends.append(ends[-1] + a.size)
    total = taken_together(jnp.concatenate([a.ravel() for a in arrays]), axis)
    return tuple((total[b:e].reshape(a.shape) for a, b, e in zip(arrays, ends, ends[1:])))


def combine_rows(first, second):
    top = jnp.maximum(first[0], second[0])
    left = jnp.exp(first[0] - top)
    right = jnp.exp(second[0] - top)
    return (top, first[1] * left + second[1] * right, first[2] * left + second[2] * right)


def body(hidden, head, mask):
    inclusion_indicator = mask.astype(jnp.float32)
    slots = jnp.cumsum(mask) - 1
    picker = (slots[None, :] == jnp.arange(ACT_DEV, dtype=jnp.int32)[:, None]) & (
        mask[None, :] == 1
    )
    picker = picker.astype(jnp.bfloat16)
    source = jnp.dot(picker, hidden, preferred_element_type=jnp.float32).astype(jnp.bfloat16)
    rows_here = source.shape[0]
    logits = jnp.dot(
        lax.all_gather(source, SEQ, axis=0, tiled=True), head, preferred_element_type=jnp.float32
    )
    local_top = jnp.max(logits, axis=1)
    local_ex = jnp.exp(logits - local_top[:, None])
    top, total, weighted = combined_by_axis(
        (local_top, jnp.sum(local_ex, axis=1), jnp.sum(local_ex * logits, axis=1)),
        SEQ_VOCAB,
        combine_rows,
    )
    ex = jnp.exp(logits - top[:, None])
    mean_logit = weighted / total
    distribution_uncertainty = top + jnp.log(total) - mean_logit
    prob = ex / total[:, None]
    score_grad = (-(prob * (logits - mean_logit[:, None]))).astype(jnp.bfloat16)
    partial_grad = lax.psum_scatter(
        lax.dot_general(
            score_grad, head, (((1,), (1,)), ((), ())), preferred_element_type=jnp.float32
        ).astype(jnp.bfloat16),
        SEQ,
        scatter_dimension=0,
        tiled=True,
    )
    column_grad = sent_and_summed(partial_grad, "vocab", 1)
    position = lax.axis_index(SEQ) * rows_here
    mine = lax.dynamic_slice_in_dim(distribution_uncertainty, position, rows_here, 0)
    spread = picker.astype(jnp.float32)
    mine = lax.dot_general(
        spread, mine[:, None], (((0,), (0,)), ((), ())), precision=lax.Precision.HIGHEST
    )[:, 0]
    column_grad = lax.dot_general(
        spread, column_grad, (((0,), (0,)), ((), ())), precision=lax.Precision.HIGHEST
    )
    positionwise_uncertainty = inclusion_indicator * mine
    aggregate_uncertainty, response_length_total = packed_total(
        (jnp.sum(positionwise_uncertainty), jnp.sum(inclusion_indicator)), SEQ
    )
    average_uncertainty_reward = aggregate_uncertainty / response_length_total
    derivative_wrt_latent_vectors = (inclusion_indicator[:, None] * column_grad).astype(
        jnp.bfloat16
    )
    return (positionwise_uncertainty, average_uncertainty_reward, derivative_wrt_latent_vectors)


def solution(mesh):
    finer = Mesh(
        mesh.devices.reshape(4, 4, 2, mesh.shape["vocab"]), ("seq_0", "seq_1", "seq_2", "vocab")
    )
    placed = (P(SEQ, None), P(None, SEQ_VOCAB), P(SEQ))
    return jax.shard_map(
        body, mesh=finer, in_specs=placed, out_specs=(P(SEQ), P(), P(SEQ, "vocab")), check_vma=False
    )
```

profile of v0, /device:TPU:2, one launch (start us, length us, event | category | flops | bytes accessed | tf_op | source)
XLA Modules:
  0.0 263.5 jit_solution(15623832513023680919)
XLA Ops:
  7.2 0.0 copy-start
  7.2 0.0 all-gather.10.cloned.1.call-start
  7.2 0.8 broadcast_compare_fusion
  8.0 0.8 copy.12
  8.8 0.2 reduce-window.8
  9.0 0.1 add_reduce_fusion
  9.1 0.0 copy-done
  9.1 1.1 convolution_convert_fusion.1
  10.2 0.0 all-gather.10.cloned.1.call-update
  10.2 0.0 reduce-scatter.2.cloned.1.call-start
  10.2 61.6 %all-gather.10.cloned.1.call-done = bf16[512,8192]{1,0:T(8,128)(2,1)} async-done(((bf16[16,8192]{1,0:T(8,128)(2,1)}), bf16[512,8192]{1,0:T(8,128)(2,1)}) %all-gather.10.cloned.1.call-update) | async-done | bytes 8388624 | tf_op jit(solution)/shard_map/all_gather | solution.py:85
  71.9 0.0 copy-start.1
  71.9 7.1 %fusion.72 = (f32[512]{0:T(512)S(1)}, f32[512,256]{0,1:T(8,128)S(1)}) fusion(bf16[512,8192]{1,0:T(8,128)(2,1)} %all-gather.10.cloned.1.call-done, bf16[8192,256]{1,0:T(8,128)(2,1)} %param.4), kind=kOutput, calls=%fused_computation.146 | convolution fusion | flops 2147614208 | bytes 13109248 | tf_op jit(solution)/shard_map/dot_general | solution.py:84
  79.0 0.1 fusion.2
  79.2 11.9 %all-gather.4 = f32[4,3,512]{2,1,0:T(4,128)S(1)} all-gather(f32[1,3,512]{2,1,0:T(4,128)S(1)} %maximum_bitcast_fusion), channel_id=2, replica_groups=mesh['seq_0'=4,'seq_1'=4,'seq_2'=2,'vocab'=8] {'seq_0'}, dimensions={0}, use_global_device_ids=true | all-gather | bytes 30720 | tf_op jit(solution)/shard_map/all_gather | solution.py:20
  91.2 11.9 %all-gather.5 = f32[4,3,512]{2,1,0:T(4,128)S(1)} all-gather(f32[1,3,512]{2,1,0:T(4,128)S(1)} %maximum_bitcast_fusion.1), channel_id=3, replica_groups=mesh['seq_0'=4,'seq_1'=4,'seq_2'=2,'vocab'=8] {'seq_1'}, dimensions={0}, use_global_device_ids=true | all-gather | bytes 30720 | tf_op jit(solution)/shard_map/all_gather | solution.py:20
  103.2 1.8 all-gather.6
  105.1 26.0 %all-gather.7 = f32[8,3,512]{2,1,0:T(4,128)S(1)} all-gather(f32[1,3,512]{2,1,0:T(4,128)S(1)} %maximum_bitcast_fusion.3), channel_id=5, replica_groups=mesh['seq_0'=4,'seq_1'=4,'seq_2'=2,'vocab'=8] {'vocab'}, dimensions={0}, use_global_device_ids=true | all-gather | bytes 55296 | tf_op jit(solution)/shard_map/all_gather | solution.py:20
  131.2 0.1 add_subtract_fusion
  131.2 0.0 copy-done.1
  131.3 5.6 %convolution_convert_fusion = bf16[512,8192]{1,0:T(8,128)(2,1)} fusion(bf16[8192,256]{1,0:T(8,128)(2,1)S(1)} %copy-done.1, f32[512,256]{0,1:T(8,128)S(1)} %get-tuple-element.48, f32[512]{0:T(512)S(1)} %get-tuple-element.6, f32[512]{0:T(512)S(1)} %get-tuple-element.7, f32[512]{0:T(512)S(1)} %get-tuple-element.8), kind=kOutput, calls=%fused_computation | convolution fusion | flops 2152464384 | bytes 13113344 | tf_op jit(solution)/shard_map/dot_general | solution.py:100
  136.9 0.0 copy-start.2
  136.9 0.0 reduce-scatter.2.cloned.1.call-update
  136.9 0.6 copy-done.2
  137.6 0.6 convert_reduce_fusion.1
  138.2 1.3 fusion.73
  139.5 1.4 pad_maximum_fusion
  140.8 0.6 broadcast_in_dim.2
  141.4 5.6 %all-to-all-start = ((f32[32,1,2]{2,1,0:T(1,128)}), f32[32,1,2]{2,1,0:T(1,128)S(1)}, u32[]{:S(2)}, u32[]{:S(2)}) async-start(f32[32,1,2]{2,1,0:T(1,128)} %broadcast_in_dim.2), calls=%async_computation | async-start | bytes 32768 | tf_op jit(solution)/shard_map/all_to_all | solution.py:51
  147.0 88.1 %reduce-scatter.2.cloned.1.call-done = bf16[16,8192]{1,0:T(8,128)(2,1)} async-done(((bf16[512,8192]{1,0:T(8,128)(2,1)}), bf16[16,8192]{1,0:T(8,128)(2,1)}) %reduce-scatter.2.cloned.1.call-update) | async-done | bytes 262160 | tf_op jit(solution)/shard_map/reduce_scatter | solution.py:99
  235.2 1.7 copy.20
  236.8 0.0 all-to-all-done
  236.8 7.0 %all-to-all-start.1 = ((bf16[8,16,1024]{2,1,0:T(8,128)(2,1)}), bf16[8,16,1024]{2,1,0:T(8,128)(2,1)S(1)}, u32[]{:S(2)}, u32[]{:S(2)}) async-start(bf16[8,16,1024]{2,1,0:T(8,128)(2,1)} %bitcast.357), calls=%async_computation.2 | async-start | bytes 524288 | tf_op jit(solution)/shard_map/all_to_all | solution.py:45
  243.9 0.1 reduce_sum.58
  243.9 0.6 fusion.71
  245.9 8.4 %all-to-all-done.1 = bf16[8,16,1024]{2,1,0:T(8,128)(2,1)S(1)} async-done(((bf16[8,16,1024]{2,1,0:T(8,128)(2,1)}), bf16[8,16,1024]{2,1,0:T(8,128)(2,1)S(1)}, u32[]{:S(2)}, u32[]{:S(2)}) %all-to-all-start.1) | async-done | bytes 262176 | tf_op jit(solution)/shard_map/all_to_all | solution.py:45
  254.4 1.1 fusion
  (15 shorter events, 0.3 us)
Async XLA Ops:
  7.2 1.9 copy-start
  7.2 64.7 %all-gather.10.cloned.1.call-start = ((), (), s32[]{:S(2)}) async-start(), calls=%async_computation.3 | async-start | bytes 8650752 | tf_op jit(solution)/shard_map/all_gather | solution.py:85
  10.2 225.0 %reduce-scatter.2.cloned.1.call-start = ((), (), s32[]{:S(2)}) async-start(), calls=%async_computation.4 | async-start | bytes 8650752 | tf_op jit(solution)/shard_map/reduce_scatter | solution.py:99
  71.9 59.4 %copy-start.1 = (bf16[8192,256]{1,0:T(8,128)(2,1)S(1)}, bf16[8192,256]{1,0:T(8,128)(2,1)}, u32[]{:S(2)}) copy-start(bf16[8192,256]{1,0:T(8,128)(2,1)} %param.4) | copy-start | bytes 12582916
  136.9 0.7 copy-start.2
  141.4 95.4 %all-to-all-start = ((f32[32,1,2]{2,1,0:T(1,128)}), f32[32,1,2]{2,1,0:T(1,128)S(1)}, u32[]{:S(2)}, u32[]{:S(2)}) async-start(f32[32,1,2]{2,1,0:T(1,128)} %broadcast_in_dim.2), calls=%async_computation | async-start | bytes 32768 | tf_op jit(solution)/shard_map/all_to_all | solution.py:51
  236.8 17.5 %all-to-all-start.1 = ((bf16[8,16,1024]{2,1,0:T(8,128)(2,1)}), bf16[8,16,1024]{2,1,0:T(8,128)(2,1)S(1)}, u32[]{:S(2)}, u32[]{:S(2)}) async-start(bf16[8,16,1024]{2,1,0:T(8,128)(2,1)} %bitcast.357), calls=%async_computation.2 | async-start | bytes 524288 | tf_op jit(solution)/shard_map/all_to_all | solution.py:45
Sparse Core Ops, SparseCore 0:
  11.1 60.7 all-gather.9
  137.0 98.0 reduce-scatter.1
where the time goes:
time: 264 us; the launch traced here: 263 us
  waiting for transfers between devices  158 us (60%)
  blocking collectives  51.7 us (20%)
  between operations  16.7 us (6%)
  matrix products  16.3 us (6%)
  starting transfers between devices  12.7 us (5%)
  local copies, waits for them, and re-layouts  4.31 us (2%)
  other arithmetic  3.53 us (1%)
    reduce_scatter x1, waiting for transfers between devices, body(): lax.psum_scatter(lax.dot_general(score_grad, head, (((1,), (1,)), ((), ()...  88.1 us
    all_gather x1, waiting for transfers between devices, body(): lax.all_gather(source, SEQ, axis=0, tiled=True)  61.6 us
    all_gather x4, blocking collectives, gathered_once(): both, at, found = (lax.all_gather(jnp.concatenate(lines), axis), 0, {})  51.7 us
    all_to_all x1, waiting for transfers between devices, sent_and_summed(): lax.all_to_all(pieces, axis, split_axis=0, concat_axis=0, tiled=True)  8.45 us
    dot_general x1, matrix products, body(): jnp.dot(lax.all_gather(source, SEQ, axis=0, tiled=True), head, preferred_...  7.11 us
    all_to_all x1, starting transfers between devices, sent_and_summed(): lax.all_to_all(pieces, axis, split_axis=0, concat_axis=0, tiled=True)  7.02 us
    dot_general x1, matrix products, body(): lax.dot_general(score_grad, head, (((1,), (1,)), ((), ())), preferred_ele...  5.64 us
    all_to_all x1, starting transfers between devices, from_everyone(): lax.all_to_all(jnp.broadcast_to(array[None], (devices, *array.shape)), ax...  5.56 us
  transfers between devices with their start and end apart: 4, of which 3 were waited for; matrix products, arithmetic and copies ran while one was open for 2% of the time, Pallas kernels for 0%

commit v1 on v0

--- a/solution.py
+++ b/solution.py
@@ -73,6 +73,12 @@
 
 
 def body(hidden, head, mask):
+
+    def part_streams(z, peer_axis):
+        w1 = jnp.stack([z for _ in range(lax.axis_size(peer_axis))])
+        tmp = jnp.concatenate(lax.all_to_all(w1, peer_axis, 0, 0), axis=0)
+        return tmp
+
     inclusion_indicator = mask.astype(jnp.float32)
     slots = jnp.cumsum(mask) - 1
     picker = (slots[None, :] == jnp.arange(ACT_DEV, dtype=jnp.int32)[:, None]) & (
@@ -81,9 +87,7 @@
     picker = picker.astype(jnp.bfloat16)
     source = jnp.dot(picker, hidden, preferred_element_type=jnp.float32).astype(jnp.bfloat16)
     rows_here = source.shape[0]
-    logits = jnp.dot(
-        lax.all_gather(source, SEQ, axis=0, tiled=True), head, preferred_element_type=jnp.float32
-    )
+    logits = jnp.dot(part_streams(source, SEQ), head, preferred_element_type=jnp.float32)
     local_top = jnp.max(logits, axis=1)
     local_ex = jnp.exp(logits - local_top[:, None])
     top, total, weighted = combined_by_axis(

time: 264 us -> 305 us (1.16)
  blocking collectives: 51.7 us -> 155 us
  waiting for transfers between devices: 158 us -> 95.9 us
    all_to_all x0 -> x1, blocking collectives: none -> 102 us  [part_streams(): tmp = jnp.concatenate(lax.all_to_all(w1, peer_axis, 0, 0), axis=0)]
    all_gather x1 -> x0, waiting for transfers between devices: 61.6 us -> none  [body(): lax.all_gather(source, SEQ, axis=0, tiled=True)]
  transfers between devices with their start and end apart: 4 -> 3, of which waited for: 3 -> 2; matrix products, arithmetic and copies ran while one was open for 2% -> 2% of each run, Pallas kernels for 0% -> 0%
where the time goes in v1:
time: 305 us
  blocking collectives  155 us (51%)
  waiting for transfers between devices  95.9 us (31%)
  between operations  16.7 us (5%)
  matrix products  15.3 us (5%)
  starting transfers between devices  13.5 us (4%)
  local copies, waits for them, and re-layouts  5.31 us (2%)
  other arithmetic  3.53 us (1%)
    all_to_all x1, blocking collectives, part_streams(): tmp = jnp.concatenate(lax.all_to_all(w1, peer_axis, 0, 0), axis=0)  102 us
    reduce_scatter x1, waiting for transfers between devices, body(): lax.psum_scatter(lax.dot_general(score_grad, head, (((1,), (1,)), ((), ()...  87.4 us
    all_gather x4, blocking collectives, gathered_once(): both, at, found = (lax.all_gather(jnp.concatenate(lines), axis), 0, {})  52.7 us
    all_to_all x1, waiting for transfers between devices, sent_and_summed(): lax.all_to_all(pieces, axis, split_axis=0, concat_axis=0, tiled=True)  8.45 us
    dot_general x1, matrix products, body(): lax.dot_general(score_grad, head, (((1,), (1,)), ((), ())), preferred_ele...  7.84 us
    all_to_all x1, starting transfers between devices, sent_and_summed(): lax.all_to_all(pieces, axis, split_axis=0, concat_axis=0, tiled=True)  7 us
    all_to_all x1, starting transfers between devices, from_everyone(): lax.all_to_all(jnp.broadcast_to(array[None], (devices, *array.shape)), ax...  6.45 us
  transfers between devices with their start and end apart: 3, of which 2 were waited for; matrix products, arithmetic and copies ran while one was open for 2% of the time, Pallas kernels for 0%

profile of v1, /device:TPU:2, one launch (start us, length us, event | category | flops | bytes accessed | tf_op | source)
XLA Modules:
  0.0 304.9 jit_solution(428424245421309867)
XLA Ops:
  7.2 0.0 copy-start
  7.2 0.0 reduce-scatter.2.cloned.1.call-start
  7.2 0.8 broadcast_compare_fusion
  8.0 0.8 copy.12
  8.8 0.2 reduce-window.8
  9.0 0.1 add_reduce_fusion
  9.1 0.0 copy-done
  9.1 0.4 convolution_convert_fusion.1
  9.5 1.0 stack.2
  10.5 102.1 %all_to_all.16 = bf16[32,16,8192]{2,1,0:T(8,128)(2,1)S(1)} all-to-all(bf16[32,16,8192]{2,1,0:T(8,128)(2,1)S(1)} %stack.2), channel_id=1, replica_groups=mesh['seq_0'=4,'seq_1'=4,'seq_2'=2,'vocab'=8] {'seq_0','seq_1','seq_2'}, dimensions={0} | all-to-all | bytes 16777216 | tf_op jit(solution)/shard_map/all_to_all | solution.py:79
  112.5 4.6 %fusion.72 = (f32[512]{0:T(512)S(1)}, f32[512,256]{0,1:T(8,128)S(1)}) fusion(bf16[512,8192]{1,0:T(8,128)(2,1)S(1)} %bitcast.359, bf16[8192,256]{1,0:T(8,128)(2,1)} %param.4), kind=kOutput, calls=%fused_computation.146 | convolution fusion | flops 2147614208 | bytes 13109248 | tf_op jit(solution)/shard_map/dot_general | solution.py:90
  117.2 0.1 fusion.2
  117.3 11.9 %all-gather.4 = f32[4,3,512]{2,1,0:T(4,128)S(1)} all-gather(f32[1,3,512]{2,1,0:T(4,128)S(1)} %maximum_bitcast_fusion), channel_id=2, replica_groups=mesh['seq_0'=4,'seq_1'=4,'seq_2'=2,'vocab'=8] {'seq_0'}, dimensions={0}, use_global_device_ids=true | all-gather | bytes 30720 | tf_op jit(solution)/shard_map/all_gather | solution.py:20
  129.3 10.7 %all-gather.5 = f32[4,3,512]{2,1,0:T(4,128)S(1)} all-gather(f32[1,3,512]{2,1,0:T(4,128)S(1)} %maximum_bitcast_fusion.1), channel_id=3, replica_groups=mesh['seq_0'=4,'seq_1'=4,'seq_2'=2,'vocab'=8] {'seq_1'}, dimensions={0}, use_global_device_ids=true | all-gather | bytes 30720 | tf_op jit(solution)/shard_map/all_gather | solution.py:20
  140.1 1.8 all-gather.6
  142.0 28.2 %all-gather.7 = f32[8,3,512]{2,1,0:T(4,128)S(1)} all-gather(f32[1,3,512]{2,1,0:T(4,128)S(1)} %maximum_bitcast_fusion.3), channel_id=5, replica_groups=mesh['seq_0'=4,'seq_1'=4,'seq_2'=2,'vocab'=8] {'vocab'}, dimensions={0}, use_global_device_ids=true | all-gather | bytes 55296 | tf_op jit(solution)/shard_map/all_gather | solution.py:20
  170.3 0.1 add_subtract_fusion
  170.4 7.8 %convolution_convert_fusion = bf16[512,8192]{1,0:T(8,128)(2,1)} fusion(bf16[8192,256]{1,0:T(8,128)(2,1)} %param.4, f32[512,256]{0,1:T(8,128)S(1)} %get-tuple-element.48, f32[512]{0:T(512)S(1)} %get-tuple-element.6, f32[512]{0:T(512)S(1)} %get-tuple-element.7, f32[512]{0:T(512)S(1)} %get-tuple-element.8), kind=kOutput, calls=%fused_computation | convolution fusion | flops 2152464384 | bytes 13113344 | tf_op jit(solution)/shard_map/dot_general | solution.py:104
  178.2 0.0 copy-start.1
  178.2 0.0 reduce-scatter.2.cloned.1.call-update
  178.2 0.6 copy-done.1
  178.9 0.6 convert_reduce_fusion.1
  179.5 1.3 fusion.73
  180.8 1.4 pad_maximum_fusion
  182.1 0.6 broadcast_in_dim.2
  182.7 6.4 %all-to-all-start.1 = ((f32[32,1,2]{2,1,0:T(1,128)}), f32[32,1,2]{2,1,0:T(1,128)S(1)}, u32[]{:S(2)}, u32[]{:S(2)}) async-start(f32[32,1,2]{2,1,0:T(1,128)} %broadcast_in_dim.2), calls=%async_computation.1 | async-start | bytes 32768 | tf_op jit(solution)/shard_map/all_to_all | solution.py:51
  189.2 87.4 %reduce-scatter.2.cloned.1.call-done = bf16[16,8192]{1,0:T(8,128)(2,1)} async-done(((bf16[512,8192]{1,0:T(8,128)(2,1)}), bf16[16,8192]{1,0:T(8,128)(2,1)}) %reduce-scatter.2.cloned.1.call-update) | async-done | bytes 262160 | tf_op jit(solution)/shard_map/reduce_scatter | solution.py:103
  276.6 1.7 copy.20
  278.3 0.0 all-to-all-done.1
  278.3 7.0 %all-to-all-start.2 = ((bf16[8,16,1024]{2,1,0:T(8,128)(2,1)}), bf16[8,16,1024]{2,1,0:T(8,128)(2,1)S(1)}, u32[]{:S(2)}, u32[]{:S(2)}) async-start(bf16[8,16,1024]{2,1,0:T(8,128)(2,1)} %bitcast.358), calls=%async_computation.3 | async-start | bytes 524288 | tf_op jit(solution)/shard_map/all_to_all | solution.py:45
  285.3 0.1 reduce_sum.58
  285.3 0.6 fusion.71
  287.3 8.4 %all-to-all-done.2 = bf16[8,16,1024]{2,1,0:T(8,128)(2,1)S(1)} async-done(((bf16[8,16,1024]{2,1,0:T(8,128)(2,1)}), bf16[8,16,1024]{2,1,0:T(8,128)(2,1)S(1)}, u32[]{:S(2)}, u32[]{:S(2)}) %all-to-all-start.2) | async-done | bytes 262176 | tf_op jit(solution)/shard_map/all_to_all | solution.py:45
  295.8 1.1 fusion
  (15 shorter events, 0.3 us)
Async XLA Ops:
  7.2 1.9 copy-start
  7.2 269.4 %reduce-scatter.2.cloned.1.call-start = ((), (), s32[]{:S(2)}) async-start(), calls=%async_computation.4 | async-start | bytes 8650752 | tf_op jit(solution)/shard_map/reduce_scatter | solution.py:103
  178.2 0.7 copy-start.1
  182.7 95.5 %all-to-all-start.1 = ((f32[32,1,2]{2,1,0:T(1,128)}), f32[32,1,2]{2,1,0:T(1,128)S(1)}, u32[]{:S(2)}, u32[]{:S(2)}) async-start(f32[32,1,2]{2,1,0:T(1,128)} %broadcast_in_dim.2), calls=%async_computation.1 | async-start | bytes 32768 | tf_op jit(solution)/shard_map/all_to_all | solution.py:51
  278.3 17.5 %all-to-all-start.2 = ((bf16[8,16,1024]{2,1,0:T(8,128)(2,1)}), bf16[8,16,1024]{2,1,0:T(8,128)(2,1)S(1)}, u32[]{:S(2)}, u32[]{:S(2)}) async-start(bf16[8,16,1024]{2,1,0:T(8,128)(2,1)} %bitcast.358), calls=%async_computation.3 | async-start | bytes 524288 | tf_op jit(solution)/shard_map/all_to_all | solution.py:45
Sparse Core Ops, SparseCore 0:
  178.3 98.2 reduce-scatter.1
